TPU v7x, 512 devices: a whole 4x4x16 slice. The times are simulated.
512 devices in a mesh: gx: 4 (over y_hi, core), gy: 16 (over z), gz: 8 (over y_lo, x).
Axes of the slice: x: 4, y: 4 (y_hi: 2, y_lo: 2; y = y_hi * 2 + y_lo), z: 16, core: 2. Of those that a mesh axis runs over, the one named last changes fastest.
Arguments:
- heat_level_grid: float32 [256, 1024, 512], P('gz', 'gy', 'gx'), may hold values from -16 to 16, as said below
- interval_first_class: int32 [1], replicated, may hold values from 0 to 95
- interval_beyond_class: int32 [1], replicated, may hold values from 128 to 256
Outputs:
- magnitude: float32 [256, 1024, 512], P('gz', 'gy', 'gx')
- histogram: float32 [256], replicated
- stats: float32 [4], replicated
Inputs may be any that keep to these rules, and one draw needn't show every extreme that they name: `heat_level_grid`: each entry is a rough value times an amplitude that is constant on blocks of 8 x 4 x 4 cells (z, y, x) and varies over a factor of 16 between blocks.
All inputs are finite; a program needn't handle non-finite values.
Results may differ from a plain program's by a relative error of at most 0.0003.
Values sent between devices are 32-bit elements; how exact they have to be, the bound alone decides.
A program may use at most 64 MiB of HBM per device.

v0:
```python
import functools

import jax
import jax.numpy as jnp
from jax import lax
from jax.experimental import pallas as pl
from jax.experimental.pallas import tpu as pltpu
from jax.sharding import PartitionSpec as P

BINS = 256
FINE = 32
COARSE = BINS // FINE
GROUPS = 8
RANGE = 12.0
COEFS = (0.8, -0.2, 4.0 / 105.0, -1.0 / 280.0)
SCALE = 840.0
TAPS = (672.0, -168.0, 32.0, -3.0)
MESH = pl.DeviceIdType.MESH
F32 = jnp.float32
BF16 = jnp.bfloat16
UNROLL = 8
EDGE = 4


def tap(distance):
    value = jnp.zeros(distance.shape, F32)
    for k, t in enumerate(TAPS, start=1):
        value = jnp.where(distance == k, t, value)
        value = jnp.where(distance == -k, -t, value)
    return value


def kernel(
    sizes,
    first_ref,
    beyond_ref,
    x_ref,
    mag_ref,
    hist_ref,
    stat_ref,
    ext,
    packed,
    from_left,
    from_right,
    band,
    rim_band,
    rim_part,
    acc,
    gather,
    in_sem,
    send_sem,
    recv_sem,
    ready_y,
    ready_z,
    all_send,
    all_recv,
):
    names = ("gx", "gy", "gz")
    nz, ny, nx = x_ref.shape
    where = {a: lax.axis_index(a) for a in names}
    total = sizes["gx"] * sizes["gy"] * sizes["gz"]

    loads = [
        pltpu.make_async_copy(
            x_ref.at[pl.ds(a, b)], ext.at[pl.ds(4 + a, b), pl.ds(8, ny)], in_sem.at[i]
        )
        for i, (a, b) in enumerate(((0, nz // 2), (nz // 2, nz - nz // 2)))
    ]
    for c in loads:
        c.start()

    def others(axis):
        n = sizes[axis]
        return [lax.rem(where[axis] + d, n) for d in range(1, n)]

    ahead = {(a, d): lax.rem(where[a] + d, sizes[a]) for a in names for d in range(sizes[a])}
    barrier = pltpu.get_barrier_semaphore()
    greeted = 0
    for a in names:
        for other in others(a):
            pl.semaphore_signal(barrier, inc=1, device_id={a: other}, device_id_type=MESH)
            greeted += 1

    row = lax.broadcasted_iota(jnp.int32, (128, 128), 0)
    col = lax.broadcasted_iota(jnp.int32, (128, 128), 1)
    diag = tap(row - col).astype(BF16)
    band[0:128, :] = diag
    band[128:256, :] = diag
    r16 = lax.broadcasted_iota(jnp.int32, (16, 128), 0)
    l16 = lax.broadcasted_iota(jnp.int32, (16, 128), 1)
    m16 = lax.rem(r16, 8)
    place = jnp.where(m16 < 4, m16 - 4, 124 + m16)
    rim_tap = tap(place - l16)
    even = jnp.where(r16 < 8, rim_tap, 0.0).astype(BF16)
    odd = jnp.where(r16 >= 8, rim_tap, 0.0).astype(BF16)
    rim_band[...] = jnp.zeros(rim_band.shape, BF16)
    for j in range(16):
        tile = odd if j % 2 else even
        base = (j // 2) * 16
        rim_band[base : base + 16, 128 * j : 128 * (j + 1)] = tile
        rim_band[128 + base : 144 + base, 128 * j : 128 * (j + 1)] = tile
    acc[...] = jnp.zeros(acc.shape, F32)

    for c in loads:
        c.wait()

    planes = nz // 16
    lane = lax.broadcasted_iota(jnp.int32, (128, 128), 1)
    rims = None
    for j in range(16):
        block = ext[4 + planes * j : 4 + planes * (j + 1), 8 : 8 + ny, :].reshape(planes * ny, 128)
        turned = pltpu.roll(block, (8 * j + 4) % 128, 1)
        rims = turned if rims is None else jnp.where(lane >= 8 * j, turned, rims)
    packed[...] = rims

    pl.semaphore_wait(barrier, greeted)

    def up(a):
        return {a: lax.rem(where[a] + 1, sizes[a])}

    def down(a):
        return {a: lax.rem(where[a] + sizes[a] - 1, sizes[a])}

    def remote(src, dst, i, device):
        return pltpu.make_async_remote_copy(
            src_ref=src,
            dst_ref=dst,
            send_sem=send_sem.at[i],
            recv_sem=recv_sem.at[i],
            device_id=device,
            device_id_type=MESH,
        )

    own = pl.ds(4, nz)
    wide = pl.ds(8, ny)
    z_low = remote(ext.at[pl.ds(nz, 4), wide], ext.at[pl.ds(0, 4), wide], 4, up("gz"))
    z_high = remote(ext.at[pl.ds(4, 4), wide], ext.at[pl.ds(nz + 4, 4), wide], 5, down("gz"))
    y_low = remote(ext.at[own, pl.ds(4 + ny, 4)], ext.at[own, pl.ds(4, 4)], 2, up("gy"))
    y_high = remote(ext.at[own, pl.ds(8, 4)], ext.at[own, pl.ds(8 + ny, 4)], 3, down("gy"))
    x_low = remote(packed, from_left, 0, up("gx"))
    x_high = remote(packed, from_right, 1, down("gx"))
    x_low.start()
    x_high.start()
    y_low.start()
    y_high.start()
    z_low.start()
    z_high.start()
    for other in others("gy"):
        pl.semaphore_signal(ready_y, inc=1, device_id={"gy": other}, device_id_type=MESH)

    x_low.wait()
    x_high.wait()
    rim = jnp.where(lax.rem(lane, 8) < 4, from_left[...], from_right[...])
    rim_hi = rim.astype(BF16)
    rim_lo = (rim - rim_hi.astype(F32)).astype(BF16)
    rim_part[...] = jnp.dot(
        jnp.concatenate([rim_hi, rim_lo], axis=1), rim_band[...], preferred_element_type=F32
    )
    lower = first_ref[0].astype(F32) - 1.0
    upper = beyond_ref[0].astype(F32)
    parity = jnp.where(lax.broadcasted_iota(jnp.int32, (16, 128), 0) >= 8, 1.0, 0.0)

    def twice(a):
        return jnp.concatenate([a, a], axis=0)

    def rates(blocks):
        sides = []
        for z, t0, nt in blocks:
            here = ext[z + 4, 8 + 8 * t0 : 8 + 8 * (t0 + nt), :]
            hi = here.astype(BF16)
            lo = (here - hi.astype(F32)).astype(BF16)
            sides.append(jnp.concatenate([hi, lo], axis=1))
        return jnp.dot(jnp.concatenate(sides, axis=0), band[...], preferred_element_type=F32)

    def plane(z, t0, nt, gx):
        y0, n = 8 + 8 * t0, 8 * nt
        rows = pl.multiple_of(lax.rem(z, planes) * ny + 8 * t0, 8)
        cols = pl.multiple_of((z // planes) * 128, 128)
        gx = (gx + rim_part[pl.ds(rows, n), pl.ds(cols, 128)]) * (1.0 / SCALE)
        gy = None
        gz = None
        for k, c in enumerate(COEFS, start=1):
            y_term = c * (ext[z + 4, y0 + k : y0 + k + n, :] - ext[z + 4, y0 - k : y0 - k + n, :])
            z_term = c * (ext[z + 4 + k, y0 : y0 + n, :] - ext[z + 4 - k, y0 : y0 + n, :])
            gy = y_term if gy is None else gy + y_term
            gz = z_term if gz is None else gz + z_term
        m = jnp.sqrt(gz * gz + gy * gy + gx * gx + 1.0) - 1.0
        mag_ref[z, 8 * t0 : 8 * (t0 + nt), :] = m
        q = jnp.clip(m * (BINS / RANGE), 0.5, BINS - 0.5) - 0.5
        low = jnp.minimum(jnp.floor(q), BINS - 2.0)
        frac = q - low
        w = jnp.clip(jnp.minimum(q - lower, upper - q), 0.0, 1.0)
        wm = w * m
        worst = m + RANGE * (1.0 - w)
        coarse = jnp.floor(low * (1.0 / FINE))
        fine = low - FINE * coarse
        frac_hi = frac.astype(BF16).astype(F32)
        frac_lo = frac - frac_hi
        left, right = [], []
        zero = jnp.zeros((16, 128), BF16)
        one = jnp.ones((16, 128), BF16)
        for i in range(nt):
            s = slice(8 * i, 8 * i + 8)
            c2 = (twice(coarse[s]) - parity).astype(BF16)
            f2 = (twice(fine[s]) - parity).astype(BF16)
            h2 = twice(frac_hi[s]).astype(BF16)
            l2 = twice(frac_lo[s]).astype(BF16)
            ones, his, los = [], [], []
            for j in range(COARSE // 2):
                hit = c2 == jnp.asarray(2 * j, BF16)
                ones.append(jnp.where(hit, one, zero))
                his.append(jnp.where(hit, h2, zero))
                los.append(jnp.where(hit, l2, zero))
            left.append(jnp.concatenate(ones + his + los, axis=0))
            right.append(
                jnp.concatenate(
                    [jnp.where(f2 == jnp.asarray(2 * j, BF16), one, zero) for j in range(FINE // 2)], axis=0
                )
            )
        fold = lambda op, a: functools.reduce(op, [a[8 * i : 8 * i + 8] for i in range(nt)])
        return left, right, fold(jnp.add, wm), fold(jnp.add, w), fold(jnp.maximum, wm), fold(jnp.minimum, worst)

    def several(blocks, carry):
        left, right = [], []
        s, n, hi, lo = carry
        gx = rates(blocks)
        start = 0
        for z, t0, nt in blocks:
            l, r, ps, pn, phi, plo = plane(z, t0, nt, gx[start : start + 8 * nt])
            start += 8 * nt
            left += l
            right += r
            s, n, hi, lo = s + ps, n + pn, jnp.maximum(hi, phi), jnp.minimum(lo, plo)
        acc[...] += lax.dot_general(
            jnp.concatenate(left, axis=1),
            jnp.concatenate(right, axis=1),
            (((1,), (1,)), ((), ())),
            preferred_element_type=F32,
        )
        return s, n, hi, lo

    zeros = jnp.zeros((8, 128), F32)
    carry = (zeros, zeros, zeros, jnp.full((8, 128), 3.0e38, F32))
    tiles = ny // 8
    inner = (nz - 8) // UNROLL
    carry = lax.fori_loop(
        0, inner, lambda t, c: several([(4 + t * UNROLL + u, 1, tiles - 2) for u in range(UNROLL)], c), carry
    )
    y_low.wait()
    y_high.wait()
    ends = [(u, t0, 1) for u in range(nz - 8) for t0 in (0, tiles - 1)]
    carry = lax.fori_loop(
        0, 1, lambda t, c: several([(4 + t * (nz - 8) + u, a, b) for u, a, b in ends], c), carry
    )
    z_low.wait()
    z_high.wait()
    pl.semaphore_wait(ready_y, sizes["gy"] - 1)
    for other in others("gz"):
        pl.semaphore_signal(ready_z, inc=1, device_id={"gz": other}, device_id_type=MESH)

    def edge(t, c):
        z = t * EDGE
        z = z + (z // 4) * (nz - 8)
        return several([(z + u, 0, tiles) for u in range(EDGE)], c)

    wsum, wcount, highest, lowest = lax.fori_loop(0, 8 // EDGE, edge, carry)

    span = COARSE * GROUPS
    rows = lax.broadcasted_iota(jnp.int32, (span, FINE * GROUPS), 0)
    cols = lax.broadcasted_iota(jnp.int32, (span, FINE * GROUPS), 1)
    keep = lax.rem(rows, GROUPS) == lax.rem(cols, GROUPS)

    def by_class(a):
        a = jnp.where(keep, a, 0.0)
        return jnp.sum(a.reshape(COARSE, GROUPS, FINE * GROUPS), axis=1)

    count = by_class(acc[0:span, :])
    part = by_class(acc[span : 2 * span, :] + acc[2 * span : 3 * span, :])
    from_row = lax.broadcasted_iota(jnp.int32, (FINE * GROUPS, 128), 0) // GROUPS
    to_lane = lax.rem(lax.broadcasted_iota(jnp.int32, (FINE * GROUPS, 128), 1), FINE)
    spread = jnp.where(from_row == to_lane, 1.0, 0.0)
    both = jnp.dot(
        jnp.concatenate([count, part], axis=0),
        spread,
        precision=lax.Precision.HIGHEST,
        preferred_element_type=F32,
    )
    r8 = lax.broadcasted_iota(jnp.int32, (16, 128), 0)
    l8 = lax.broadcasted_iota(jnp.int32, (16, 128), 1)
    both = jnp.where(lax.rem(r8, 4) == l8 // FINE, both, 0.0)
    quad = [jnp.sum(both[4 * i : 4 * i + 4], axis=0, keepdims=True) for i in range(4)]
    lane1 = lax.broadcasted_iota(jnp.int32, (1, 128), 1)
    turned = [pltpu.roll(quad[2], 1, 1), pltpu.roll(quad[3], 1, 1)]
    row0 = quad[0] - quad[2] + jnp.where(lane1 == 0, turned[1], turned[0])
    row1 = quad[1] - quad[3] + jnp.where(lane1 == 0, turned[0], turned[1])

    def all_of(op, a):
        return op(op(a, axis=0, keepdims=True), axis=1, keepdims=True)

    row2 = jnp.where(
        lane1 == 0,
        all_of(jnp.min, lowest),
        jnp.where(
            lane1 == 1,
            all_of(jnp.max, highest),
            jnp.where(lane1 == 2, all_of(jnp.sum, wsum), all_of(jnp.sum, wcount)),
        ),
    )
    me = (where["gx"] * sizes["gy"] + where["gy"]) * sizes["gz"] + where["gz"]
    gather[me] = jnp.concatenate([row0, row1, row2, jnp.zeros((1, 128), F32)], axis=0)

    pl.semaphore_wait(ready_z, sizes["gz"] - 1)

    def spread_to(gx, gy, gz):
        pltpu.make_async_remote_copy(
            src_ref=gather.at[me],
            dst_ref=gather.at[me],
            send_sem=all_send,
            recv_sem=all_recv,
            device_id={"gx": gx, "gy": gy, "gz": gz},
            device_id_type=MESH,
        ).start()

    def spread_out(t, c):
        other = lax.rem(me + t, total)
        spread_to(
            other // (sizes["gy"] * sizes["gz"]),
            lax.rem(other // sizes["gz"], sizes["gy"]),
            lax.rem(other, sizes["gz"]),
        )
        return c

    if total > 64:
        lax.fori_loop(1, total, spread_out, 0)
    else:
        far = lambda n: sorted(range(n), key=lambda d: -min(d, n - d))
        for dy in far(sizes["gy"]):
            for dz in far(sizes["gz"]):
                for dx in far(sizes["gx"]):
                    if dx or dy or dz:
                        spread_to(*[ahead[a, d] for a, d in (("gx", dx), ("gy", dy), ("gz", dz))])
    rest = gather.at[pl.ds(0, total - 1)]
    every = pltpu.make_async_remote_copy(
        src_ref=rest,
        dst_ref=rest,
        send_sem=all_send,
        recv_sem=all_recv,
        device_id=up("gx"),
        device_id_type=MESH,
    )
    every.wait()
    parts = gather[...]
    summed = jnp.sum(parts, axis=0)
    smallest = jnp.min(parts, axis=0)
    largest = jnp.max(parts, axis=0)
    cells = nz * ny * nx * total
    hist_ref[...] = summed[0:2] * (BINS / cells)
    stat_ref[...] = jnp.where(
        lane1 == 0,
        smallest[2:3],
        jnp.where(lane1 == 1, largest[2:3], summed[2:3] * (1.0 / cells)),
    )[:, 0:4]


def finish(mag_ref, hist_ref, stat_ref, mag_out, hist_out, stat_out, sem):
    copy = pltpu.make_async_copy(mag_ref, mag_out, sem)
    copy.start()
    hist_out[...] = hist_ref[...]
    stat_out[...] = stat_ref[...]
    copy.wait()


def solution(mesh):
    sizes = dict(mesh.shape)
    total = sizes["gx"] * sizes["gy"] * sizes["gz"]

    def on_device(grid, first, beyond):
        nz, ny, nx = grid.shape
        vmem = pl.BlockSpec(memory_space=pltpu.VMEM)
        hbm = pl.BlockSpec(memory_space=pltpu.HBM)
        packed_rows = nz * ny // 16
        magnitude, histogram, stats = pl.pallas_call(
            functools.partial(kernel, sizes),
            out_shape=(
                jax.ShapeDtypeStruct(grid.shape, F32),
                jax.ShapeDtypeStruct((2, 128), F32),
                jax.ShapeDtypeStruct((1, 4), F32),
            ),
            in_specs=[pl.BlockSpec(memory_space=pltpu.SMEM), pl.BlockSpec(memory_space=pltpu.SMEM), hbm],
            out_specs=(vmem, vmem, vmem),
            scratch_shapes=[
                pltpu.VMEM((nz + 8, ny + 16, nx), F32),
                pltpu.VMEM((packed_rows, 128), F32),
                pltpu.VMEM((packed_rows, 128), F32),
                pltpu.VMEM((packed_rows, 128), F32),
                pltpu.VMEM((256, 128), BF16),
                pltpu.VMEM((256, 2048), BF16),
                pltpu.VMEM((packed_rows, 2048), F32),
                pltpu.VMEM((3 * COARSE * GROUPS, FINE * GROUPS), F32),
                pltpu.VMEM((total, 4, 128), F32),
                pltpu.SemaphoreType.DMA((2,)),
                pltpu.SemaphoreType.DMA((6,)),
                pltpu.SemaphoreType.DMA((6,)),
                pltpu.SemaphoreType.REGULAR,
                pltpu.SemaphoreType.REGULAR,
                pltpu.SemaphoreType.DMA,
                pltpu.SemaphoreType.DMA,
            ],
            compiler_params=pltpu.CompilerParams(
                collective_id=0, has_side_effects=True, vmem_limit_bytes=32768 * 1024
            ),
        )(first, beyond, grid)
        magnitude, histogram, stats = pl.pallas_call(
            finish,
            out_shape=(
                jax.ShapeDtypeStruct(grid.shape, F32),
                jax.ShapeDtypeStruct((2, 128), F32),
                jax.ShapeDtypeStruct((1, 4), F32),
            ),
            in_specs=[vmem, vmem, vmem],
            out_specs=(hbm, vmem, vmem),
            scratch_shapes=[pltpu.SemaphoreType.DMA],
            compiler_params=pltpu.CompilerParams(vmem_limit_bytes=4 * 1024 * 1024),
        )(magnitude, histogram, stats)
        return magnitude, histogram.reshape(BINS), stats.reshape(4)

    return jax.shard_map(
        on_device,
        mesh=mesh,
        in_specs=(P("gz", "gy", "gx"), P(), P()),
        out_specs=(P("gz", "gy", "gx"), P(), P()),
        check_vma=False,
    )
```

profile of v0, /device:TPU:1, one launch (start us, length us, event | category | flops | bytes accessed | tf_op | source)
XLA Modules:
  0.0 87.1 jit_solution(1858006838108293411)
XLA Ops:
  1.9 0.0 copy-start
  1.9 1.2 %copy-done = f32[32,64,128]{2,1,0:T(8,128)S(1)} copy-done((f32[32,64,128]{2,1,0:T(8,128)S(1)}, f32[32,64,128]{2,1,0:T(8,128)}, u32[]{:S(2)}) %copy-start) | copy-done | bytes 1048600
  3.1 82.4 %shard_map.58 = (f32[32,64,128]{2,1,0:T(8,128)S(1)}, f32[2,128]{1,0:T(2,128)S(1)}, f32[1,4]{1,0:T(1,128)S(1)}) custom-call(s32[1]{0:T(128)S(6)} %copy.6.first_ref, s32[1]{0:T(128)S(6)} %copy.7.beyond_ref, f32[32,64,128]{2,1,0:T(8,128)S(1)} %copy-done), custom_call_target="tpu_custom_call" | custom-call | tf_op jit(solution)/shard_map/pallas_call | solution.py:382
  85.5 1.5 %shard_map.59 = (f32[32,64,128]{2,1,0:T(8,128)}, f32[2,128]{1,0:T(2,128)}, f32[1,4]{1,0:T(1,128)}) custom-call(f32[32,64,128]{2,1,0:T(8,128)S(1)} %get-tuple-element.9.mag_ref, f32[2,128]{1,0:T(2,128)S(1)} %get-tuple-element.10.hist_ref, f32[1,4]{1,0:T(1,128)S(1)} %get-tuple-element.11.stat_ref), custom_call_target="tpu_custom_call" | custom-call | tf_op jit(solution)/shard_map/pallas_call | solution.py:413
Async XLA Ops:
  1.9 1.2 %copy-start = (f32[32,64,128]{2,1,0:T(8,128)S(1)}, f32[32,64,128]{2,1,0:T(8,128)}, u32[]{:S(2)}) copy-start(f32[32,64,128]{2,1,0:T(8,128)} %x_ref.1) | copy-start | bytes 3145732
where the time goes:
time: 87.9 us; the launch traced here: 87.1 us
  Pallas kernels  83.9 us (95%)
  between operations  1.94 us (2%)
  local copies, waits for them, and re-layouts  1.22 us (1%)
    pallas_call x1, Pallas kernels, on_device(): pl.pallas_call(functools.partial(kernel, sizes), out_shape=(jax.ShapeDtyp...  82.4 us

commit v1 on v0

--- a/solution.py
+++ b/solution.py
@@ -46,7 +46,8 @@
     rim_band,
     rim_part,
     acc,
-    gather,
+    gather_near,
+    gather_far,
     in_sem,
     send_sem,
     recv_sem,
@@ -58,7 +59,9 @@
     names = ("gx", "gy", "gz")
     nz, ny, nx = x_ref.shape
     where = {a: lax.axis_index(a) for a in names}
-    total = sizes["gx"] * sizes["gy"] * sizes["gz"]
+    near_total = sizes["gx"] * sizes["gz"]
+    far_total = sizes["gy"]
+    total = near_total * far_total
 
     loads = [
         pltpu.make_async_copy(
@@ -69,17 +72,31 @@
     for c in loads:
         c.start()
 
-    def others(axis):
-        n = sizes[axis]
-        return [lax.rem(where[axis] + d, n) for d in range(1, n)]
-
     ahead = {(a, d): lax.rem(where[a] + d, sizes[a]) for a in names for d in range(sizes[a])}
+
+    def signal(sem, axis, distance):
+        steps = sorted({distance % sizes[axis], -distance % sizes[axis]} - {0})
+        for d in steps:
+            pl.semaphore_signal(sem, inc=1, device_id={axis: ahead[axis, d]}, device_id_type=MESH)
+        return len(steps)
+
     barrier = pltpu.get_barrier_semaphore()
     greeted = 0
-    for a in names:
-        for other in others(a):
-            pl.semaphore_signal(barrier, inc=1, device_id={a: other}, device_id_type=MESH)
-            greeted += 1
+    for d in range(1, sizes["gx"] // 2 + 1):
+        greeted += signal(barrier, "gx", d)
+    greeted += signal(barrier, "gz", 1)
+    greeted += signal(barrier, "gy", 1)
+    z_hops = [1 << i for i in range(max(1, (sizes["gz"] // 2).bit_length()))]
+    y_hops = [1 << i for i in range(max(1, (sizes["gy"] // 4).bit_length()))]
+    heard = {}
+
+    def tell(axis, sems, hops, i):
+        if i < len(hops):
+            heard[axis, i] = signal(sems.at[i], axis, hops[i])
+
+    def hear(axis, sems, hops, i):
+        if i < len(hops):
+            pl.semaphore_wait(sems.at[i], heard[axis, i])
 
     row = lax.broadcasted_iota(jnp.int32, (128, 128), 0)
     col = lax.broadcasted_iota(jnp.int32, (128, 128), 1)
@@ -145,8 +162,8 @@
     y_high.start()
     z_low.start()
     z_high.start()
-    for other in others("gy"):
-        pl.semaphore_signal(ready_y, inc=1, device_id={"gy": other}, device_id_type=MESH)
+    tell("gz", ready_z, z_hops, 0)
+    tell("gy", ready_y, y_hops, 0)
 
     x_low.wait()
     x_high.wait()
@@ -248,15 +265,20 @@
     )
     y_low.wait()
     y_high.wait()
+    hear("gz", ready_z, z_hops, 0)
+    hear("gy", ready_y, y_hops, 0)
+    tell("gz", ready_z, z_hops, 1)
+    tell("gy", ready_y, y_hops, 1)
     ends = [(u, t0, 1) for u in range(nz - 8) for t0 in (0, tiles - 1)]
     carry = lax.fori_loop(
         0, 1, lambda t, c: several([(4 + t * (nz - 8) + u, a, b) for u, a, b in ends], c), carry
     )
     z_low.wait()
     z_high.wait()
-    pl.semaphore_wait(ready_y, sizes["gy"] - 1)
-    for other in others("gz"):
-        pl.semaphore_signal(ready_z, inc=1, device_id={"gz": other}, device_id_type=MESH)
+    hear("gz", ready_z, z_hops, 1)
+    hear("gy", ready_y, y_hops, 1)
+    tell("gz", ready_z, z_hops, 2)
+    tell("gy", ready_y, y_hops, 2)
 
     def edge(t, c):
         z = t * EDGE
@@ -306,60 +328,58 @@
             jnp.where(lane1 == 2, all_of(jnp.sum, wsum), all_of(jnp.sum, wcount)),
         ),
     )
-    me = (where["gx"] * sizes["gy"] + where["gy"]) * sizes["gz"] + where["gz"]
-    gather[me] = jnp.concatenate([row0, row1, row2, jnp.zeros((1, 128), F32)], axis=0)
-
-    pl.semaphore_wait(ready_z, sizes["gz"] - 1)
-
-    def spread_to(gx, gy, gz):
+    near = where["gx"] * sizes["gz"] + where["gz"]
+    far = where["gy"]
+    by_distance = lambda n: sorted(range(n), key=lambda d: -min(d, n - d))
+
+    def share(buffer, slot, row, devices, i):
+        buffer[slot] = row
+        for device in devices:
+            pltpu.make_async_remote_copy(
+                src_ref=buffer.at[slot],
+                dst_ref=buffer.at[slot],
+                send_sem=all_send.at[i],
+                recv_sem=all_recv.at[i],
+                device_id=device,
+                device_id_type=MESH,
+            ).start()
+        rest = buffer.at[pl.ds(0, len(devices))]
         pltpu.make_async_remote_copy(
-            src_ref=gather.at[me],
-            dst_ref=gather.at[me],
-            send_sem=all_send,
-            recv_sem=all_recv,
-            device_id={"gx": gx, "gy": gy, "gz": gz},
+            src_ref=rest,
+            dst_ref=rest,
+            send_sem=all_send.at[i],
+            recv_sem=all_recv.at[i],
+            device_id=up("gx"),
             device_id_type=MESH,
-        ).start()
-
-    def spread_out(t, c):
-        other = lax.rem(me + t, total)
-        spread_to(
-            other // (sizes["gy"] * sizes["gz"]),
-            lax.rem(other // sizes["gz"], sizes["gy"]),
-            lax.rem(other, sizes["gz"]),
-        )
-        return c
-
-    if total > 64:
-        lax.fori_loop(1, total, spread_out, 0)
-    else:
-        far = lambda n: sorted(range(n), key=lambda d: -min(d, n - d))
-        for dy in far(sizes["gy"]):
-            for dz in far(sizes["gz"]):
-                for dx in far(sizes["gx"]):
-                    if dx or dy or dz:
-                        spread_to(*[ahead[a, d] for a, d in (("gx", dx), ("gy", dy), ("gz", dz))])
-    rest = gather.at[pl.ds(0, total - 1)]
-    every = pltpu.make_async_remote_copy(
-        src_ref=rest,
-        dst_ref=rest,
-        send_sem=all_send,
-        recv_sem=all_recv,
-        device_id=up("gx"),
-        device_id_type=MESH,
-    )
-    every.wait()
-    parts = gather[...]
-    summed = jnp.sum(parts, axis=0)
-    smallest = jnp.min(parts, axis=0)
-    largest = jnp.max(parts, axis=0)
+        ).wait()
+        parts = buffer[...]
+        summed = jnp.sum(parts, axis=0)
+        smallest = jnp.min(parts[:, 2:3], axis=0)
+        largest = jnp.max(parts[:, 2:3], axis=0)
+        stat = jnp.where(lane1 == 0, smallest, jnp.where(lane1 == 1, largest, summed[2:3]))
+        return jnp.concatenate([summed[0:2], stat, jnp.zeros((1, 128), F32)], axis=0)
+
+    hear("gz", ready_z, z_hops, 2)
+    row = jnp.concatenate([row0, row1, row2, jnp.zeros((1, 128), F32)], axis=0)
+    row = share(
+        gather_near,
+        near,
+        row,
+        [
+            {"gx": ahead["gx", dx], "gz": ahead["gz", dz]}
+            for dz in by_distance(sizes["gz"])
+            for dx in by_distance(sizes["gx"])
+            if dx or dz
+        ],
+        0,
+    )
+    hear("gy", ready_y, y_hops, 2)
+    row = share(
+        gather_far, far, row, [{"gy": ahead["gy", dy]} for dy in by_distance(sizes["gy"]) if dy], 1
+    )
     cells = nz * ny * nx * total
-    hist_ref[...] = summed[0:2] * (BINS / cells)
-    stat_ref[...] = jnp.where(
-        lane1 == 0,
-        smallest[2:3],
-        jnp.where(lane1 == 1, largest[2:3], summed[2:3] * (1.0 / cells)),
-    )[:, 0:4]
+    hist_ref[...] = row[0:2] * (BINS / cells)
+    stat_ref[...] = jnp.where(lane1 < 2, row[2:3], row[2:3] * (1.0 / cells))[:, 0:4]
 
 
 def finish(mag_ref, hist_ref, stat_ref, mag_out, hist_out, stat_out, sem):
@@ -372,8 +392,6 @@
 
 def solution(mesh):
     sizes = dict(mesh.shape)
-    total = sizes["gx"] * sizes["gy"] * sizes["gz"]
-
     def on_device(grid, first, beyond):
         nz, ny, nx = grid.shape
         vmem = pl.BlockSpec(memory_space=pltpu.VMEM)
@@ -397,14 +415,15 @@
                 pltpu.VMEM((256, 2048), BF16),
                 pltpu.VMEM((packed_rows, 2048), F32),
                 pltpu.VMEM((3 * COARSE * GROUPS, FINE * GROUPS), F32),
-                pltpu.VMEM((total, 4, 128), F32),
+                pltpu.VMEM((sizes["gx"] * sizes["gz"], 4, 128), F32),
+                pltpu.VMEM((sizes["gy"], 4, 128), F32),
                 pltpu.SemaphoreType.DMA((2,)),
                 pltpu.SemaphoreType.DMA((6,)),
                 pltpu.SemaphoreType.DMA((6,)),
-                pltpu.SemaphoreType.REGULAR,
-                pltpu.SemaphoreType.REGULAR,
-                pltpu.SemaphoreType.DMA,
-                pltpu.SemaphoreType.DMA,
+                pltpu.SemaphoreType.REGULAR((3,)),
+                pltpu.SemaphoreType.REGULAR((3,)),
+                pltpu.SemaphoreType.DMA((2,)),
+                pltpu.SemaphoreType.DMA((2,)),
             ],
             compiler_params=pltpu.CompilerParams(
                 collective_id=0, has_side_effects=True, vmem_limit_bytes=32768 * 1024

time: 87.9 us -> 46.5 us (0.53)
  Pallas kernels: 83.9 us -> 43.1 us
    pallas_call x1, Pallas kernels: 82.4 us -> 41.6 us  [on_device(): pl.pallas_call(functools.partial(kernel, sizes), out_shape=(jax.ShapeDtyp...]
where the time goes in v1:
time: 46.5 us; the launch traced here: 46.3 us
  Pallas kernels  43.1 us (93%)
  between operations  1.94 us (4%)
  local copies, waits for them, and re-layouts  1.22 us (3%)
    pallas_call x1, Pallas kernels, on_device(): pl.pallas_call(functools.partial(kernel, sizes), out_shape=(jax.ShapeDtyp...  41.6 us
    pallas_call x1, Pallas kernels, on_device(): pl.pallas_call(finish, out_shape=(jax.ShapeDtypeStruct(grid.shape, F32),...  1.54 us
    unnamed x2, local copies, waits for them, and re-layouts  1.22 us

profile of v1, /device:TPU:1, one launch (start us, length us, event | category | flops | bytes accessed | tf_op | source)
XLA Modules:
  0.0 46.3 jit_solution(1703489898668835243)
XLA Ops:
  1.9 0.0 copy-start
  1.9 1.2 %copy-done = f32[32,64,128]{2,1,0:T(8,128)S(1)} copy-done((f32[32,64,128]{2,1,0:T(8,128)S(1)}, f32[32,64,128]{2,1,0:T(8,128)}, u32[]{:S(2)}) %copy-start) | copy-done | bytes 1048600
  3.1 41.6 %shard_map.58 = (f32[32,64,128]{2,1,0:T(8,128)S(1)}, f32[2,128]{1,0:T(2,128)S(1)}, f32[1,4]{1,0:T(1,128)S(1)}) custom-call(s32[1]{0:T(128)S(6)} %copy.6.first_ref, s32[1]{0:T(128)S(6)} %copy.7.beyond_ref, f32[32,64,128]{2,1,0:T(8,128)S(1)} %copy-done), custom_call_target="tpu_custom_call" | custom-call | tf_op jit(solution)/shard_map/pallas_call | solution.py:400
  44.7 1.5 %shard_map.59 = (f32[32,64,128]{2,1,0:T(8,128)}, f32[2,128]{1,0:T(2,128)}, f32[1,4]{1,0:T(1,128)}) custom-call(f32[32,64,128]{2,1,0:T(8,128)S(1)} %get-tuple-element.9.mag_ref, f32[2,128]{1,0:T(2,128)S(1)} %get-tuple-element.10.hist_ref, f32[1,4]{1,0:T(1,128)S(1)} %get-tuple-element.11.stat_ref), custom_call_target="tpu_custom_call" | custom-call | tf_op jit(solution)/shard_map/pallas_call | solution.py:432
Async XLA Ops:
  1.9 1.2 %copy-start = (f32[32,64,128]{2,1,0:T(8,128)S(1)}, f32[32,64,128]{2,1,0:T(8,128)}, u32[]{:S(2)}) copy-start(f32[32,64,128]{2,1,0:T(8,128)} %x_ref.1) | copy-start | bytes 3145732

commit v2 on v1

v2 whole, which is shorter than its diff:
```python
import functools

import jax
import jax.numpy as jnp
from jax import lax
from jax.experimental import pallas as pl
from jax.experimental.pallas import tpu as pltpu
from jax.sharding import PartitionSpec as P

BINS = 256
FINE = 24
COARSE = 12
GROUPS = 8
RANGE = 12.0
COEFS = (0.8, -0.2, 4.0 / 105.0, -1.0 / 280.0)
SCALE = 840.0
TAPS = (672.0, -168.0, 32.0, -3.0)
MESH = pl.DeviceIdType.MESH
F32 = jnp.float32
BF16 = jnp.bfloat16
SPAN = COARSE * GROUPS
WIDTH = FINE * GROUPS
BIG = 3.0e38
VMEM_KIB = 32768
DOTS = 2
HALVES = 2


def tap(distance):
    value = jnp.zeros(distance.shape, F32)
    for k, t in enumerate(TAPS, start=1):
        value = jnp.where(distance == k, t, value)
        value = jnp.where(distance == -k, -t, value)
    return value


def iota(shape, axis):
    return lax.broadcasted_iota(jnp.int32, shape, axis)


def kernel(
    sizes,
    first_ref,
    beyond_ref,
    x_ref,
    mag_ref,
    hist_ref,
    stat_ref,
    ext,
    packed,
    to_right,
    to_left,
    from_left,
    from_right,
    cross,
    rim_m,
    slope,
    square,
    rim_slope,
    rim_square,
    acc,
    unit,
    gather_near,
    gather_far,
    in_sem,
    send_sem,
    recv_sem,
    ready_y,
    ready_z,
    all_send,
    all_recv,
):
    names = ("gx", "gy", "gz")
    nz, ny, nx = x_ref.shape
    tiles = ny // 8
    where = {a: lax.axis_index(a) for a in names}
    total = sizes["gx"] * sizes["gy"] * sizes["gz"]
    ahead = {(a, d): lax.rem(where[a] + d, sizes[a]) for a in names for d in range(sizes[a])}

    loads = [
        pltpu.make_async_copy(
            x_ref.at[pl.ds(a, b - a)], ext.at[pl.ds(4 + a, b - a), pl.ds(8, ny)], in_sem.at[i]
        )
        for i, (a, b) in enumerate(((0, nz // 2), (nz // 2, nz)))
    ]
    for c in loads:
        c.start()

    def signal(sem, axis, distance):
        steps = sorted({distance % sizes[axis], -distance % sizes[axis]} - {0})
        for d in steps:
            pl.semaphore_signal(sem, inc=1, device_id={axis: ahead[axis, d]}, device_id_type=MESH)
        return len(steps)

    barrier = pltpu.get_barrier_semaphore()
    greeted = 0
    for d in range(1, sizes["gx"] // 2 + 1):
        greeted += signal(barrier, "gx", d)
    greeted += signal(barrier, "gz", 1)
    greeted += signal(barrier, "gy", 1)
    z_hops = [1 << i for i in range(max(1, (sizes["gz"] // 2).bit_length()))]
    y_hops = [1 << i for i in range(max(1, (sizes["gy"] // 4).bit_length()))]
    heard = {}

    def tell(axis, sems, hops, i):
        if i < len(hops):
            heard[axis, i] = signal(sems.at[i], axis, hops[i])

    def hear(axis, sems, hops, i):
        if i < len(hops):
            pl.semaphore_wait(sems.at[i], heard[axis, i])

    def up(a):
        return {a: ahead[a, 1]}

    def down(a):
        return {a: ahead[a, sizes[a] - 1]}

    def remote(src, dst, i, device):
        return pltpu.make_async_remote_copy(
            src_ref=src,
            dst_ref=dst,
            send_sem=send_sem.at[i],
            recv_sem=recv_sem.at[i],
            device_id=device,
            device_id_type=MESH,
        )

    own = pl.ds(4, nz)
    wide = pl.ds(8, ny)

    def z_pair(low, high, i):
        return (
            remote(ext.at[pl.ds(nz + low, 2), wide], ext.at[pl.ds(low, 2), wide], i, up("gz")),
            remote(ext.at[pl.ds(high, 2), wide], ext.at[pl.ds(nz + high, 2), wide], i + 1, down("gz")),
        )

    z_near = z_pair(2, 4, 4)
    z_far = z_pair(0, 6, 6)
    y_low = remote(ext.at[own, pl.ds(4 + ny, 4)], ext.at[own, pl.ds(4, 4)], 2, up("gy"))
    y_high = remote(ext.at[own, pl.ds(8, 4)], ext.at[own, pl.ds(8 + ny, 4)], 3, down("gy"))
    x_low = remote(to_right, from_left, 0, up("gx"))
    x_high = remote(to_left, from_right, 1, down("gx"))

    planes = 2
    rows = planes * ny
    half = rows // 2
    lane = iota((8, 128), 1)
    outer = jnp.logical_or(lane < 4, lane >= nx - 4)
    low_four = lax.rem(iota((half, 128), 1), 8) < 4

    def turn(a, j):
        return pltpu.roll(a, (8 * j + 4) % 128, 1)

    def back(a, j):
        return pltpu.roll(a, (124 - 8 * j) % 128, 1)

    gathered = [None] * (planes * tiles)
    for n, c in enumerate(loads):
        c.wait()
        groups = nz // planes // len(loads)
        for i in range(planes * tiles):
            u, t = i // tiles, i % tiles
            for j in range(n * groups, (n + 1) * groups):
                turned = turn(ext[4 + planes * j + u, 8 + 8 * t : 16 + 8 * t, :], j)
                gathered[i] = turned if j == 0 else jnp.where(lane >= 8 * j, turned, gathered[i])
    for i in range(planes * tiles):
        packed[8 * i : 8 * i + 8, :] = gathered[i]
    upper_half, lower_half = packed[0:half, :], packed[half:rows, :]
    to_right[...] = jnp.where(low_four, upper_half, pltpu.roll(lower_half, 4, 1))
    to_left[...] = jnp.where(low_four, pltpu.roll(upper_half, 124, 1), lower_half)

    pl.semaphore_wait(barrier, greeted)
    x_low.start()
    x_high.start()
    y_low.start()
    y_high.start()
    tell("gz", ready_z, z_hops, 0)
    tell("gy", ready_y, y_hops, 0)

    from_step = iota((WIDTH, BINS), 0) // GROUPS
    bin_of = iota((WIDTH, BINS), 1)
    digit = jnp.floor((bin_of.astype(F32) + 0.5) * (1.0 / FINE)).astype(jnp.int32)
    to_step = bin_of - FINE * digit
    single = jnp.where(to_step == FINE - 1, 1.0, 2.0)
    mix = jnp.where(from_step == to_step, single, jnp.where(jnp.abs(from_step - to_step) == 1, -1.0, 0.0))
    const = jnp.where(to_step == 0, 0.0, jnp.where(lax.rem(to_step, 2) == 1, -single, 2.0))
    r, c = iota((128, 128), 0), iota((128, 128), 1)
    same = jnp.logical_and(r // 8 == c // 8, (lax.rem(r, 8) < 4) != (lax.rem(c, 8) < 4))
    taps = jnp.where(same, tap(r - c), 0.0).astype(BF16)
    cross[...] = jnp.concatenate([taps, taps], axis=0)
    unit[...] = jnp.where(from_step == 0, const, mix).astype(BF16)
    for c in (*z_near, *z_far):
        c.start()

    lower = first_ref[...].astype(F32) - 1.0
    upper = beyond_ref[...].astype(F32)
    parity = jnp.where(iota((16, 128), 0) >= 8, 1.0, 0.0)
    lane16 = iota((16, 128), 1)
    never = jnp.full((16, 128), 1024.0, F32)
    inner_parity = jnp.where(jnp.logical_or(lane16 < 4, lane16 >= nx - 4), never, parity).astype(BF16)
    parity = parity.astype(BF16)
    zero = jnp.zeros((16, 128), BF16)
    one = jnp.ones((16, 128), BF16)

    def twice(a):
        return jnp.concatenate([a, a], axis=0).astype(BF16)

    def rates(z, t):
        y = 8 + 8 * t
        here = ext[z + 4, y : y + 8, :]
        gx = gy = gz = None
        for k, c in enumerate(COEFS, start=1):
            x_term = c * (pltpu.roll(here, 128 - k, 1) - pltpu.roll(here, k, 1))
            y_term = c * (ext[z + 4, y + k : y + k + 8, :] - ext[z + 4, y - k : y - k + 8, :])
            z_term = c * (ext[z + 4 + k, y : y + 8, :] - ext[z + 4 - k, y : y + 8, :])
            gx = x_term if gx is None else gx + x_term
            gy = y_term if gy is None else gy + y_term
            gz = z_term if gz is None else gz + z_term
        return gx, gy * gy + gz * gz

    def length(gx, rest):
        s = (rest + gx * gx) + 1.0
        return s * lax.rsqrt(s) - 1.0

    def classes(m, offset):
        q = jnp.clip(m * (BINS / RANGE) - 0.5, 0.0, BINS - 1.0)
        low = jnp.minimum(jnp.floor(q), BINS - 2.0)
        w = jnp.clip(jnp.minimum(q - lower, upper - q), 0.0, 1.0)
        coarse = jnp.floor(low * (1.000001 / FINE))
        c2 = twice(coarse) - offset
        f2 = twice(low - FINE * coarse) - parity
        h2 = twice(q - low)
        ones, parts = [], []
        for j in range(COARSE // 2):
            hit = c2 == jnp.asarray(2 * j, BF16)
            ones.append(jnp.where(hit, one, zero))
            parts.append(jnp.where(hit, h2, zero))
        steps = [jnp.minimum(f2, parity - one)]
        steps += [jnp.minimum(f2, jnp.asarray(2 * j, BF16)) for j in range(1, FINE // 2)]
        wm = w * m
        stats = (wm, w, wm, m - RANGE * w)
        return jnp.concatenate(ones + parts, axis=0), jnp.concatenate(steps, axis=0), stats

    def merge(a, b):
        return (a[0] + b[0], a[1] + b[1], jnp.maximum(a[2], b[2]), jnp.minimum(a[3], b[3]))

    def tally_up(items, fresh=False):
        share_of = len(items) // 2
        for i in range(2):
            part = items[i * share_of : (i + 1) * share_of]
            left = jnp.concatenate([a for a, _, _ in part], axis=1)
            right = jnp.concatenate([b for _, b, _ in part], axis=1)
            product = lax.dot_general(left, right, (((1,), (1,)), ((), ())), preferred_element_type=F32)
            if fresh:
                acc[i] = product
            else:
                acc[i] += product
        return functools.reduce(merge, [s for _, _, s in items])

    def deferred(z, t):
        gx, rest = rates(z, t)
        at = (z, slice(8 * t, 8 * t + 8), slice(None))
        slope[at] = gx
        square[at] = rest
        m = length(gx, rest)
        mag_ref[at] = m
        return classes(m, inner_parity)

    def fold(groups, span):
        for i in [u * tiles + t for u in range(planes) for t in span]:
            u, t = i // tiles, i % tiles
            for whole, kept in ((slope, rim_slope), (square, rim_square)):
                out = None
                for first, last in groups:
                    run = None
                    for j in range(first, last):
                        turned = turn(whole[planes * j + u, 8 * t : 8 * t + 8, :], j)
                        run = turned if run is None else jnp.where(lane >= 8 * j, turned, run)
                    if len(groups) == 1:
                        out = run
                    elif out is None:
                        out = jnp.where(lane < 8 * last, run, kept[8 * i : 8 * i + 8, :])
                    else:
                        out = jnp.where(lane >= 8 * first, run, out)
                kept[8 * i : 8 * i + 8, :] = out

    inside = list(range(4, nz - 4))
    count = nz // planes
    inner = [tally_up([deferred(z, t) for z in inside for t in range(1, tiles - 1)], True)]
    fold([(2, count - 2)], range(1, tiles - 1))

    hear("gz", ready_z, z_hops, 0)
    hear("gy", ready_y, y_hops, 0)
    tell("gz", ready_z, z_hops, 1)
    tell("gy", ready_y, y_hops, 1)
    y_low.wait()
    y_high.wait()
    inner.append(tally_up([deferred(z, t) for z in inside for t in (0, tiles - 1)]))
    fold([(2, count - 2)], (0, tiles - 1))
    for c in z_near:
        c.wait()
    hear("gz", ready_z, z_hops, 1)
    hear("gy", ready_y, y_hops, 1)
    tell("gz", ready_z, z_hops, 2)
    tell("gy", ready_y, y_hops, 2)
    inner.append(tally_up([deferred(z, t) for z in (2, 3, nz - 4, nz - 3) for t in range(tiles)]))
    for c in z_far:
        c.wait()
    inner.append(tally_up([deferred(z, t) for z in (0, 1, nz - 2, nz - 1) for t in range(tiles)]))
    fold([(0, 2), (count - 2, count)], range(tiles))
    inner = functools.reduce(merge, inner)

    x_low.wait()
    x_high.wait()
    left_rim, right_rim = from_left[...], from_right[...]
    extra = (
        jnp.concatenate(
            [
                jnp.where(low_four, left_rim, pltpu.roll(right_rim, 4, 1)),
                jnp.where(low_four, pltpu.roll(left_rim, 124, 1), right_rim),
            ],
            axis=0,
        )
        - packed[...]
    )
    extra_hi = extra.astype(BF16)
    extra_lo = (extra - extra_hi.astype(F32)).astype(BF16)
    corr = jnp.dot(
        jnp.concatenate([extra_hi, extra_lo], axis=1), cross[...], preferred_element_type=F32
    ) * (1.0 / SCALE)
    rim = []
    for i in range(planes * tiles):
        at = slice(8 * i, 8 * i + 8)
        m = length(rim_slope[at, :] + corr[at], rim_square[at, :])
        rim_m[at, :] = m
        rim.append(classes(m, parity))
    rim = tally_up(rim)
    tally = acc[0] + acc[1]

    def only(keep, s):
        return (
            jnp.where(keep, s[0], 0.0),
            jnp.where(keep, s[1], 0.0),
            jnp.where(keep, s[2], 0.0),
            jnp.where(keep, s[3], BIG),
        )

    wsum, wcount, highest, lowest = functools.reduce(
        merge, [only(jnp.logical_not(outer), inner), rim]
    )

    keep = iota((GROUPS, WIDTH), 0) == lax.rem(iota((GROUPS, WIDTH), 1), GROUPS)

    def by_class(a):
        return jnp.sum(jnp.where(keep[None], a.reshape(COARSE, GROUPS, WIDTH), 0.0), axis=1)

    sums = jnp.concatenate([by_class(tally[0:SPAN, :]), by_class(tally[SPAN : 2 * SPAN, :])], axis=0)
    high = sums.astype(BF16)
    rest = sums - high.astype(F32)
    middle_bits = rest.astype(BF16)
    low_bits = (rest - middle_bits.astype(F32)).astype(BF16)
    three = jnp.dot(
        jnp.concatenate([high.astype(F32), middle_bits.astype(F32), low_bits.astype(F32)], axis=0).astype(BF16),
        unit[...],
        preferred_element_type=F32,
    )
    n = 2 * COARSE
    both = (three[2 * n : 3 * n] + three[n : 2 * n]) + three[0:n]
    place = iota((2 * COARSE, BINS), 1).astype(F32)
    digit = jnp.floor((place + 0.5) * (1.0 / FINE)).astype(jnp.int32)
    both = jnp.where(lax.rem(iota((2 * COARSE, BINS), 0), COARSE) == digit, both, 0.0)
    low_sum = jnp.sum(both[0:COARSE, :], axis=0, keepdims=True)
    part = jnp.sum(both[COARSE : 2 * COARSE, :], axis=0, keepdims=True)
    lane1 = iota((1, 128), 1)
    turned = [pltpu.roll(part[:, 0:128], 1, 1), pltpu.roll(part[:, 128:256], 1, 1)]
    row0 = low_sum[:, 0:128] - part[:, 0:128] + jnp.where(lane1 == 0, turned[1], turned[0])
    row1 = low_sum[:, 128:256] - part[:, 128:256] + jnp.where(lane1 == 0, turned[0], turned[1])

    def all_of(op, a):
        return op(op(a, axis=0, keepdims=True), axis=1, keepdims=True)

    row2 = jnp.where(
        lane1 == 0,
        all_of(jnp.min, lowest) + RANGE,
        jnp.where(
            lane1 == 1,
            all_of(jnp.max, highest),
            jnp.where(lane1 == 2, all_of(jnp.sum, wsum), all_of(jnp.sum, wcount)),
        ),
    )
    near = where["gx"] * sizes["gz"] + where["gz"]
    far = where["gy"]
    by_distance = lambda n: sorted(range(n), key=lambda d: -min(d, n - d))

    def share(buffer, slot, devices, i, meanwhile=lambda: None):
        for device in devices:
            pltpu.make_async_remote_copy(
                src_ref=buffer.at[slot],
                dst_ref=buffer.at[slot],
                send_sem=all_send.at[i],
                recv_sem=all_recv.at[i],
                device_id=device,
                device_id_type=MESH,
            ).start()
        others = buffer.at[pl.ds(0, len(devices))]
        arrival = pltpu.make_async_remote_copy(
            src_ref=others,
            dst_ref=others,
            send_sem=all_send.at[i],
            recv_sem=all_recv.at[i],
            device_id=up("gx"),
            device_id_type=MESH,
        )
        meanwhile()
        arrival.wait()
        parts = buffer[...]
        summed = jnp.sum(parts, axis=0)
        smallest = jnp.min(parts[:, 2:3], axis=0)
        largest = jnp.max(parts[:, 2:3], axis=0)
        stat = jnp.where(lane1 == 0, smallest, jnp.where(lane1 == 1, largest, summed[2:3]))
        return jnp.concatenate([summed[0:2], stat, jnp.zeros((1, 128), F32)], axis=0)

    def put_rims():
        for i in range(planes * tiles):
            u, t = i // tiles, i % tiles
            m = rim_m[8 * i : 8 * i + 8, :]
            for j in range(count):
                at = (planes * j + u, slice(8 * t, 8 * t + 8), slice(None))
                mag_ref[at] = jnp.where(outer, back(m, j), mag_ref[at])

    gather_near[near] = jnp.concatenate([row0, row1, row2, jnp.zeros((1, 128), F32)], axis=0)
    hear("gz", ready_z, z_hops, 2)
    row = share(
        gather_near,
        near,
        [
            {"gx": ahead["gx", dx], "gz": ahead["gz", dz]}
            for dz in by_distance(sizes["gz"])
            for dx in by_distance(sizes["gx"])
            if dx or dz
        ],
        0,
        put_rims,
    )
    gather_far[far] = row
    hear("gy", ready_y, y_hops, 2)
    row = share(gather_far, far, [{"gy": ahead["gy", dy]} for dy in by_distance(sizes["gy"]) if dy], 1)
    cells = nz * ny * nx * total
    hist_ref[...] = row[0:2] * (BINS / cells)
    stat_ref[...] = jnp.where(lane1 < 2, row[2:3], row[2:3] * (1.0 / cells))[:, 0:4]


def finish(mag_ref, hist_ref, stat_ref, mag_out, hist_out, stat_out, sem):
    copy = pltpu.make_async_copy(mag_ref, mag_out, sem)
    copy.start()
    hist_out[...] = hist_ref[...]
    stat_out[...] = stat_ref[...]
    copy.wait()


def solution(mesh):
    sizes = dict(mesh.shape)

    def on_device(grid, first, beyond):
        nz, ny, nx = grid.shape
        vmem = pl.BlockSpec(memory_space=pltpu.VMEM)
        hbm = pl.BlockSpec(memory_space=pltpu.HBM)
        results = (
            jax.ShapeDtypeStruct(grid.shape, F32),
            jax.ShapeDtypeStruct((2, 128), F32),
            jax.ShapeDtypeStruct((1, 4), F32),
        )
        magnitude, histogram, stats = pl.pallas_call(
            functools.partial(kernel, sizes),
            out_shape=results,
            in_specs=[vmem, vmem, hbm],
            out_specs=(vmem, vmem, vmem),
            scratch_shapes=[
                pltpu.VMEM((nz + 8, ny + 16, nx), F32),
                pltpu.VMEM((2 * ny, 128), F32),
                pltpu.VMEM((ny, 128), F32),
                pltpu.VMEM((ny, 128), F32),
                pltpu.VMEM((ny, 128), F32),
                pltpu.VMEM((ny, 128), F32),
                pltpu.VMEM((256, 128), BF16),
                pltpu.VMEM((2 * ny, 128), F32),
                pltpu.VMEM((nz, ny, nx), F32),
                pltpu.VMEM((nz, ny, nx), F32),
                pltpu.VMEM((2 * ny, 128), F32),
                pltpu.VMEM((2 * ny, 128), F32),
                pltpu.VMEM((2, 2 * SPAN, WIDTH), F32),
                pltpu.VMEM((WIDTH, BINS), BF16),
                pltpu.VMEM((sizes["gx"] * sizes["gz"], 4, 128), F32),
                pltpu.VMEM((sizes["gy"], 4, 128), F32),
                pltpu.SemaphoreType.DMA((2,)),
                pltpu.SemaphoreType.DMA((8,)),
                pltpu.SemaphoreType.DMA((8,)),
                pltpu.SemaphoreType.REGULAR((3,)),
                pltpu.SemaphoreType.REGULAR((3,)),
                pltpu.SemaphoreType.DMA((2,)),
                pltpu.SemaphoreType.DMA((2,)),
            ],
            compiler_params=pltpu.CompilerParams(
                collective_id=0, has_side_effects=True, vmem_limit_bytes=VMEM_KIB * 1024
            ),
        )(first.reshape(1, 1), beyond.reshape(1, 1), pltpu.with_memory_space_constraint(grid, pltpu.HBM))
        magnitude, histogram, stats = pl.pallas_call(
            finish,
            out_shape=results,
            in_specs=[vmem, vmem, vmem],
            out_specs=(hbm, vmem, vmem),
            scratch_shapes=[pltpu.SemaphoreType.DMA],
            compiler_params=pltpu.CompilerParams(vmem_limit_bytes=4 * 1024 * 1024),
        )(magnitude, histogram, stats)
        return magnitude, histogram.reshape(BINS), stats.reshape(4)

    return jax.shard_map(
        on_device,
        mesh=mesh,
        in_specs=(P("gz", "gy", "gx"), P(), P()),
        out_specs=(P("gz", "gy", "gx"), P(), P()),
        check_vma=False,
    )
```

time: 46.5 us -> 37.3 us (0.80)
  Pallas kernels: 43.1 us -> 35.2 us
  local copies, waits for them, and re-layouts: 1.22 us -> 0 us
    pallas_call x2, Pallas kernels: 43.1 us -> 35.2 us  [the longest x1 33.6 us: on_device(): pl.pallas_call(functools.partial(kernel, sizes), out_shape=results, in_sp...]
    unnamed x2 -> x0, local copies, waits for them, and re-layouts: 1.22 us -> none
where the time goes in v2:
time: 37.3 us; the launch traced here: 37.1 us
  Pallas kernels  35.2 us (94%)
  between operations  1.93 us (5%)
    pallas_call x1, Pallas kernels, on_device(): pl.pallas_call(functools.partial(kernel, sizes), out_shape=results, in_sp...  33.6 us
    pallas_call x1, Pallas kernels, on_device(): pl.pallas_call(finish, out_shape=results, in_specs=[vmem, vmem, vmem], ou...  1.54 us

profile of v2, /device:TPU:1, one launch (start us, length us, event | category | flops | bytes accessed | tf_op | source)
XLA Modules:
  0.0 37.1 jit_solution(17232354949584506881)
XLA Ops:
  1.9 33.6 %shard_map.58 = (f32[32,64,128]{2,1,0:T(8,128)S(1)}, f32[2,128]{1,0:T(2,128)S(1)}, f32[1,4]{1,0:T(1,128)S(1)}) custom-call(s32[1,1]{1,0:T(1,128)} %bitcast.4.first_ref, s32[1,1]{1,0:T(1,128)} %bitcast.5.beyond_ref, f32[32,64,128]{2,1,0:T(8,128)} %x_ref.1), custom_call_target="tpu_custom_call" | custom-call | tf_op jit(solution)/shard_map/pallas_call | solution.py:474
  35.6 1.5 %shard_map.59 = (f32[32,64,128]{2,1,0:T(8,128)}, f32[2,128]{1,0:T(2,128)}, f32[1,4]{1,0:T(1,128)}) custom-call(f32[32,64,128]{2,1,0:T(8,128)S(1)} %get-tuple-element.9.mag_ref, f32[2,128]{1,0:T(2,128)S(1)} %get-tuple-element.10.hist_ref, f32[1,4]{1,0:T(1,128)S(1)} %get-tuple-element.11.stat_ref), custom_call_target="tpu_custom_call" | custom-call | tf_op jit(solution)/shard_map/pallas_call | solution.py:508

commit v3 on v2

--- a/solution.py
+++ b/solution.py
@@ -52,6 +52,10 @@
     to_left,
     from_left,
     from_right,
+    to_above,
+    to_below,
+    from_below,
+    from_above,
     cross,
     rim_m,
     slope,
@@ -81,33 +85,33 @@
         pltpu.make_async_copy(
             x_ref.at[pl.ds(a, b - a)], ext.at[pl.ds(4 + a, b - a), pl.ds(8, ny)], in_sem.at[i]
         )
-        for i, (a, b) in enumerate(((0, nz // 2), (nz // 2, nz)))
+        for i, (a, b) in enumerate(((0, 4), (nz - 4, nz), (4, nz // 2), (nz // 2, nz - 4)))
     ]
     for c in loads:
         c.start()
 
-    def signal(sem, axis, distance):
-        steps = sorted({distance % sizes[axis], -distance % sizes[axis]} - {0})
+    def signal(sem, axis, distances):
+        n = sizes[axis]
+        steps = sorted({step % n for d in distances for step in (d, -d)} - {0})
         for d in steps:
             pl.semaphore_signal(sem, inc=1, device_id={axis: ahead[axis, d]}, device_id_type=MESH)
         return len(steps)
 
     barrier = pltpu.get_barrier_semaphore()
-    greeted = 0
-    for d in range(1, sizes["gx"] // 2 + 1):
-        greeted += signal(barrier, "gx", d)
-    greeted += signal(barrier, "gz", 1)
-    greeted += signal(barrier, "gy", 1)
-    z_hops = [1 << i for i in range(max(1, (sizes["gz"] // 2).bit_length()))]
-    y_hops = [1 << i for i in range(max(1, (sizes["gy"] // 4).bit_length()))]
+    greeted = (
+        signal(barrier, "gx", range(1, sizes["gx"]))
+        + signal(barrier, "gz", (1, 2))
+        + signal(barrier, "gy", (1, 2))
+    )
+    z_hops = ((1, 2), range(3, sizes["gz"] // 2 + 1))
+    y_hops = ((2,), (4,))
     heard = {}
 
     def tell(axis, sems, hops, i):
-        if i < len(hops):
-            heard[axis, i] = signal(sems.at[i], axis, hops[i])
-
-    def hear(axis, sems, hops, i):
-        if i < len(hops):
+        heard[axis, i] = signal(sems.at[i], axis, hops[i])
+
+    def hear(axis, sems, i):
+        if heard[axis, i]:
             pl.semaphore_wait(sems.at[i], heard[axis, i])
 
     def up(a):
@@ -126,19 +130,15 @@
             device_id_type=MESH,
         )
 
-    own = pl.ds(4, nz)
+    own = slice(4, 4 + nz)
     wide = pl.ds(8, ny)
 
-    def z_pair(low, high, i):
-        return (
-            remote(ext.at[pl.ds(nz + low, 2), wide], ext.at[pl.ds(low, 2), wide], i, up("gz")),
-            remote(ext.at[pl.ds(high, 2), wide], ext.at[pl.ds(nz + high, 2), wide], i + 1, down("gz")),
-        )
-
-    z_near = z_pair(2, 4, 4)
-    z_far = z_pair(0, 6, 6)
-    y_low = remote(ext.at[own, pl.ds(4 + ny, 4)], ext.at[own, pl.ds(4, 4)], 2, up("gy"))
-    y_high = remote(ext.at[own, pl.ds(8, 4)], ext.at[own, pl.ds(8 + ny, 4)], 3, down("gy"))
+    z_sends = (
+        remote(ext.at[pl.ds(nz, 4), wide], ext.at[pl.ds(0, 4), wide], 4, up("gz")),
+        remote(ext.at[pl.ds(4, 4), wide], ext.at[pl.ds(nz + 4, 4), wide], 5, down("gz")),
+    )
+    y_low = remote(to_above, from_below, 2, up("gy"))
+    y_high = remote(to_below, from_above, 3, down("gy"))
     x_low = remote(to_right, from_left, 0, up("gx"))
     x_high = remote(to_left, from_right, 1, down("gx"))
 
@@ -155,24 +155,15 @@
     def back(a, j):
         return pltpu.roll(a, (124 - 8 * j) % 128, 1)
 
-    gathered = [None] * (planes * tiles)
-    for n, c in enumerate(loads):
-        c.wait()
-        groups = nz // planes // len(loads)
-        for i in range(planes * tiles):
-            u, t = i // tiles, i % tiles
-            for j in range(n * groups, (n + 1) * groups):
-                turned = turn(ext[4 + planes * j + u, 8 + 8 * t : 16 + 8 * t, :], j)
-                gathered[i] = turned if j == 0 else jnp.where(lane >= 8 * j, turned, gathered[i])
-    for i in range(planes * tiles):
-        packed[8 * i : 8 * i + 8, :] = gathered[i]
-    upper_half, lower_half = packed[0:half, :], packed[half:rows, :]
-    to_right[...] = jnp.where(low_four, upper_half, pltpu.roll(lower_half, 4, 1))
-    to_left[...] = jnp.where(low_four, pltpu.roll(upper_half, 124, 1), lower_half)
-
+    loads[0].wait()
+    loads[1].wait()
     pl.semaphore_wait(barrier, greeted)
-    x_low.start()
-    x_high.start()
+    for c in z_sends:
+        c.start()
+    loads[2].wait()
+    loads[3].wait()
+    to_above[...] = ext[own, 4 + ny : 8 + ny, :]
+    to_below[...] = ext[own, 8:12, :]
     y_low.start()
     y_high.start()
     tell("gz", ready_z, z_hops, 0)
@@ -190,8 +181,6 @@
     taps = jnp.where(same, tap(r - c), 0.0).astype(BF16)
     cross[...] = jnp.concatenate([taps, taps], axis=0)
     unit[...] = jnp.where(from_step == 0, const, mix).astype(BF16)
-    for c in (*z_near, *z_far):
-        c.start()
 
     lower = first_ref[...].astype(F32) - 1.0
     upper = beyond_ref[...].astype(F32)
@@ -206,18 +195,28 @@
     def twice(a):
         return jnp.concatenate([a, a], axis=0).astype(BF16)
 
-    def rates(z, t):
+    def slant(pairs):
+        total_ = None
+        for c, (ahead_, behind) in zip(COEFS, pairs):
+            term = c * (ahead_ - behind)
+            total_ = term if total_ is None else total_ + term
+        return total_
+
+    steps = range(1, len(COEFS) + 1)
+
+    def along_x(z, t):
+        here = ext[z + 4, 8 + 8 * t : 16 + 8 * t, :]
+        return slant([(pltpu.roll(here, 128 - k, 1), pltpu.roll(here, k, 1)) for k in steps])
+
+    def along_y(z, t):
         y = 8 + 8 * t
-        here = ext[z + 4, y : y + 8, :]
-        gx = gy = gz = None
-        for k, c in enumerate(COEFS, start=1):
-            x_term = c * (pltpu.roll(here, 128 - k, 1) - pltpu.roll(here, k, 1))
-            y_term = c * (ext[z + 4, y + k : y + k + 8, :] - ext[z + 4, y - k : y - k + 8, :])
-            z_term = c * (ext[z + 4 + k, y : y + 8, :] - ext[z + 4 - k, y : y + 8, :])
-            gx = x_term if gx is None else gx + x_term
-            gy = y_term if gy is None else gy + y_term
-            gz = z_term if gz is None else gz + z_term
-        return gx, gy * gy + gz * gz
+        g = slant([(ext[z + 4, y + k : y + k + 8, :], ext[z + 4, y - k : y - k + 8, :]) for k in steps])
+        return g * g
+
+    def along_z(z, t):
+        y = slice(8 + 8 * t, 16 + 8 * t)
+        g = slant([(ext[z + 4 + k, y, :], ext[z + 4 - k, y, :]) for k in steps])
+        return g * g
 
     def length(gx, rest):
         s = (rest + gx * gx) + 1.0
@@ -236,11 +235,11 @@
             hit = c2 == jnp.asarray(2 * j, BF16)
             ones.append(jnp.where(hit, one, zero))
             parts.append(jnp.where(hit, h2, zero))
-        steps = [jnp.minimum(f2, parity - one)]
-        steps += [jnp.minimum(f2, jnp.asarray(2 * j, BF16)) for j in range(1, FINE // 2)]
+        ladder = [jnp.minimum(f2, parity - one)]
+        ladder += [jnp.minimum(f2, jnp.asarray(2 * j, BF16)) for j in range(1, FINE // 2)]
         wm = w * m
         stats = (wm, w, wm, m - RANGE * w)
-        return jnp.concatenate(ones + parts, axis=0), jnp.concatenate(steps, axis=0), stats
+        return jnp.concatenate(ones + parts, axis=0), jnp.concatenate(ladder, axis=0), stats
 
     def merge(a, b):
         return (a[0] + b[0], a[1] + b[1], jnp.maximum(a[2], b[2]), jnp.minimum(a[3], b[3]))
@@ -258,14 +257,29 @@
                 acc[i] += product
         return functools.reduce(merge, [s for _, _, s in items])
 
-    def deferred(z, t):
-        gx, rest = rates(z, t)
-        at = (z, slice(8 * t, 8 * t + 8), slice(None))
-        slope[at] = gx
+    def place_of(z, t):
+        return (z, slice(8 * t, 8 * t + 8), slice(None))
+
+    def deferred(z, t, known=None, *parts):
+        at = place_of(z, t)
+        if known is None:
+            gx, rest = along_x(z, t), None
+            slope[at] = gx
+        else:
+            gx, rest = slope[at], square[at] if known else None
+        for part in parts:
+            g = part(z, t)
+            rest = g if rest is None else rest + g
         square[at] = rest
         m = length(gx, rest)
         mag_ref[at] = m
         return classes(m, inner_parity)
+
+    def prepare(z, t, part):
+        at = place_of(z, t)
+        slope[at] = along_x(z, t)
+        if part is not None:
+            square[at] = part(z, t)
 
     def fold(groups, span):
         for i in [u * tiles + t for u in range(planes) for t in span]:
@@ -287,27 +301,54 @@
 
     inside = list(range(4, nz - 4))
     count = nz // planes
-    inner = [tally_up([deferred(z, t) for z in inside for t in range(1, tiles - 1)], True)]
+    outside = [z for z in range(nz) if z not in inside]
+    for t in range(tiles):
+        edge_row = t in (0, tiles - 1)
+        for z in inside if edge_row else ():
+            prepare(z, t, along_z)
+        for z in outside:
+            prepare(z, t, None if edge_row else along_y)
+    gathered = [None] * (planes * tiles)
+    for i in range(planes * tiles):
+        u, t = i // tiles, i % tiles
+        for j in range(nz // planes):
+            turned = turn(ext[4 + planes * j + u, 8 + 8 * t : 16 + 8 * t, :], j)
+            gathered[i] = turned if j == 0 else jnp.where(lane >= 8 * j, turned, gathered[i])
+        packed[8 * i : 8 * i + 8, :] = gathered[i]
+    upper_half, lower_half = packed[0:half, :], packed[half:rows, :]
+    to_right[...] = jnp.where(low_four, upper_half, pltpu.roll(lower_half, 4, 1))
+    to_left[...] = jnp.where(low_four, pltpu.roll(upper_half, 124, 1), lower_half)
+    x_low.start()
+    x_high.start()
+
+    inner = [
+        tally_up([deferred(z, t, None, along_y, along_z) for z in inside for t in range(1, tiles - 1)], True)
+    ]
     fold([(2, count - 2)], range(1, tiles - 1))
 
-    hear("gz", ready_z, z_hops, 0)
-    hear("gy", ready_y, y_hops, 0)
+    hear("gz", ready_z, 0)
+    hear("gy", ready_y, 0)
     tell("gz", ready_z, z_hops, 1)
     tell("gy", ready_y, y_hops, 1)
     y_low.wait()
     y_high.wait()
-    inner.append(tally_up([deferred(z, t) for z in inside for t in (0, tiles - 1)]))
+    ext[own, 4:8, :] = from_below[...]
+    ext[own, 8 + ny : 12 + ny, :] = from_above[...]
+    inner.append(tally_up([deferred(z, t, True, along_y) for z in inside for t in (0, tiles - 1)]))
     fold([(2, count - 2)], (0, tiles - 1))
-    for c in z_near:
+    for c in z_sends:
         c.wait()
-    hear("gz", ready_z, z_hops, 1)
-    hear("gy", ready_y, y_hops, 1)
-    tell("gz", ready_z, z_hops, 2)
-    tell("gy", ready_y, y_hops, 2)
-    inner.append(tally_up([deferred(z, t) for z in (2, 3, nz - 4, nz - 3) for t in range(tiles)]))
-    for c in z_far:
-        c.wait()
-    inner.append(tally_up([deferred(z, t) for z in (0, 1, nz - 2, nz - 1) for t in range(tiles)]))
+    inner.append(
+        tally_up(
+            [
+                deferred(z, t, False, along_y, along_z)
+                if t in (0, tiles - 1)
+                else deferred(z, t, True, along_z)
+                for z in outside
+                for t in range(tiles)
+            ]
+        )
+    )
     fold([(0, 2), (count - 2, count)], range(tiles))
     inner = functools.reduce(merge, inner)
 
@@ -419,7 +460,7 @@
         smallest = jnp.min(parts[:, 2:3], axis=0)
         largest = jnp.max(parts[:, 2:3], axis=0)
         stat = jnp.where(lane1 == 0, smallest, jnp.where(lane1 == 1, largest, summed[2:3]))
-        return jnp.concatenate([summed[0:2], stat, jnp.zeros((1, 128), F32)], axis=0)
+        return jnp.concatenate([summed[0:2], stat], axis=0)
 
     def put_rims():
         for i in range(planes * tiles):
@@ -429,8 +470,8 @@
                 at = (planes * j + u, slice(8 * t, 8 * t + 8), slice(None))
                 mag_ref[at] = jnp.where(outer, back(m, j), mag_ref[at])
 
-    gather_near[near] = jnp.concatenate([row0, row1, row2, jnp.zeros((1, 128), F32)], axis=0)
-    hear("gz", ready_z, z_hops, 2)
+    gather_near[near] = jnp.concatenate([row0, row1, row2], axis=0)
+    hear("gz", ready_z, 1)
     row = share(
         gather_near,
         near,
@@ -444,19 +485,20 @@
         put_rims,
     )
     gather_far[far] = row
-    hear("gy", ready_y, y_hops, 2)
+    hear("gy", ready_y, 1)
     row = share(gather_far, far, [{"gy": ahead["gy", dy]} for dy in by_distance(sizes["gy"]) if dy], 1)
     cells = nz * ny * nx * total
     hist_ref[...] = row[0:2] * (BINS / cells)
     stat_ref[...] = jnp.where(lane1 < 2, row[2:3], row[2:3] * (1.0 / cells))[:, 0:4]
 
 
-def finish(mag_ref, hist_ref, stat_ref, mag_out, hist_out, stat_out, sem):
-    copy = pltpu.make_async_copy(mag_ref, mag_out, sem)
-    copy.start()
-    hist_out[...] = hist_ref[...]
-    stat_out[...] = stat_ref[...]
-    copy.wait()
+def finish(*refs):
+    results, outs, sems = refs[0:3], refs[3:6], refs[6]
+    copies = [pltpu.make_async_copy(a, b, sems.at[i]) for i, (a, b) in enumerate(zip(results, outs))]
+    for copy in copies:
+        copy.start()
+    for copy in copies:
+        copy.wait()
 
 
 def solution(mesh):
@@ -483,6 +525,10 @@
                 pltpu.VMEM((ny, 128), F32),
                 pltpu.VMEM((ny, 128), F32),
                 pltpu.VMEM((ny, 128), F32),
+                pltpu.VMEM((nz, 4, nx), F32),
+                pltpu.VMEM((nz, 4, nx), F32),
+                pltpu.VMEM((nz, 4, nx), F32),
+                pltpu.VMEM((nz, 4, nx), F32),
                 pltpu.VMEM((256, 128), BF16),
                 pltpu.VMEM((2 * ny, 128), F32),
                 pltpu.VMEM((nz, ny, nx), F32),
@@ -491,13 +537,13 @@
                 pltpu.VMEM((2 * ny, 128), F32),
                 pltpu.VMEM((2, 2 * SPAN, WIDTH), F32),
                 pltpu.VMEM((WIDTH, BINS), BF16),
-                pltpu.VMEM((sizes["gx"] * sizes["gz"], 4, 128), F32),
-                pltpu.VMEM((sizes["gy"], 4, 128), F32),
-                pltpu.SemaphoreType.DMA((2,)),
-                pltpu.SemaphoreType.DMA((8,)),
-                pltpu.SemaphoreType.DMA((8,)),
-                pltpu.SemaphoreType.REGULAR((3,)),
-                pltpu.SemaphoreType.REGULAR((3,)),
+                pltpu.VMEM((sizes["gx"] * sizes["gz"], 3, 128), F32),
+                pltpu.VMEM((sizes["gy"], 3, 128), F32),
+                pltpu.SemaphoreType.DMA((4,)),
+                pltpu.SemaphoreType.DMA((6,)),
+                pltpu.SemaphoreType.DMA((6,)),
+                pltpu.SemaphoreType.REGULAR((2,)),
+                pltpu.SemaphoreType.REGULAR((2,)),
                 pltpu.SemaphoreType.DMA((2,)),
                 pltpu.SemaphoreType.DMA((2,)),
             ],
@@ -509,8 +555,8 @@
             finish,
             out_shape=results,
             in_specs=[vmem, vmem, vmem],
-            out_specs=(hbm, vmem, vmem),
-            scratch_shapes=[pltpu.SemaphoreType.DMA],
+            out_specs=(hbm, hbm, hbm),
+            scratch_shapes=[pltpu.SemaphoreType.DMA((3,))],
             compiler_params=pltpu.CompilerParams(vmem_limit_bytes=4 * 1024 * 1024),
         )(magnitude, histogram, stats)
         return magnitude, histogram.reshape(BINS), stats.reshape(4)

time: 37.3 us -> 36.4 us (0.976)
  Pallas kernels: 35.2 us -> 34.3 us
    pallas_call x1, Pallas kernels: 1.54 us -> 1 us  [on_device(): pl.pallas_call(finish, out_shape=results, in_specs=[vmem, vmem, vmem], ou...]
where the time goes in v3:
time: 36.4 us; the launch traced here: 36.3 us
  Pallas kernels  34.3 us (94%)
  between operations  1.93 us (5%)
    pallas_call x1, Pallas kernels, on_device(): pl.pallas_call(functools.partial(kernel, sizes), out_shape=results, in_sp...  33.3 us
    pallas_call x1, Pallas kernels, on_device(): pl.pallas_call(finish, out_shape=results, in_specs=[vmem, vmem, vmem], ou...  1 us

profile of v3, /device:TPU:1, one launch (start us, length us, event | category | flops | bytes accessed | tf_op | source)
XLA Modules:
  0.0 36.3 jit_solution(9827932101644882887)
XLA Ops:
  1.9 33.3 %shard_map.58 = (f32[32,64,128]{2,1,0:T(8,128)S(1)}, f32[2,128]{1,0:T(2,128)S(1)}, f32[1,4]{1,0:T(1,128)S(1)}) custom-call(s32[1,1]{1,0:T(1,128)} %bitcast.4.first_ref, s32[1,1]{1,0:T(1,128)} %bitcast.5.beyond_ref, f32[32,64,128]{2,1,0:T(8,128)} %x_ref.1), custom_call_target="tpu_custom_call" | custom-call | tf_op jit(solution)/shard_map/pallas_call | solution.py:516
  35.3 1.0 %shard_map.59 = (f32[32,64,128]{2,1,0:T(8,128)}, f32[2,128]{1,0:T(2,128)}, f32[1,4]{1,0:T(1,128)}) custom-call(f32[32,64,128]{2,1,0:T(8,128)S(1)} %get-tuple-element.9.refs_0_, f32[2,128]{1,0:T(2,128)S(1)} %get-tuple-element.10.refs_1_, f32[1,4]{1,0:T(1,128)S(1)} %get-tuple-element.11.refs_2_), custom_call_target="tpu_custom_call" | custom-call | tf_op jit(solution)/shard_map/pallas_call | solution.py:554

commit v4 on v3

--- a/solution.py
+++ b/solution.py
@@ -101,10 +101,10 @@
     greeted = (
         signal(barrier, "gx", range(1, sizes["gx"]))
         + signal(barrier, "gz", (1, 2))
-        + signal(barrier, "gy", (1, 2))
+        + signal(barrier, "gy", (1,))
     )
     z_hops = ((1, 2), range(3, sizes["gz"] // 2 + 1))
-    y_hops = ((2,), (4,))
+    y_hops = ((1,), (2,), (4,))
     heard = {}
 
     def tell(axis, sems, hops, i):
@@ -133,10 +133,13 @@
     own = slice(4, 4 + nz)
     wide = pl.ds(8, ny)
 
-    z_sends = (
-        remote(ext.at[pl.ds(nz, 4), wide], ext.at[pl.ds(0, 4), wide], 4, up("gz")),
-        remote(ext.at[pl.ds(4, 4), wide], ext.at[pl.ds(nz + 4, 4), wide], 5, down("gz")),
-    )
+    def z_pair(low, high, i):
+        return (
+            remote(ext.at[pl.ds(nz + low, 2), wide], ext.at[pl.ds(low, 2), wide], i, up("gz")),
+            remote(ext.at[pl.ds(high, 2), wide], ext.at[pl.ds(nz + high, 2), wide], i + 1, down("gz")),
+        )
+
+    z_near, z_far = z_pair(2, 4, 4), z_pair(0, 6, 6)
     y_low = remote(to_above, from_below, 2, up("gy"))
     y_high = remote(to_below, from_above, 3, down("gy"))
     x_low = remote(to_right, from_left, 0, up("gx"))
@@ -158,7 +161,7 @@
     loads[0].wait()
     loads[1].wait()
     pl.semaphore_wait(barrier, greeted)
-    for c in z_sends:
+    for c in (*z_near, *z_far):
         c.start()
     loads[2].wait()
     loads[3].wait()
@@ -169,18 +172,22 @@
     tell("gz", ready_z, z_hops, 0)
     tell("gy", ready_y, y_hops, 0)
 
-    from_step = iota((WIDTH, BINS), 0) // GROUPS
-    bin_of = iota((WIDTH, BINS), 1)
-    digit = jnp.floor((bin_of.astype(F32) + 0.5) * (1.0 / FINE)).astype(jnp.int32)
-    to_step = bin_of - FINE * digit
-    single = jnp.where(to_step == FINE - 1, 1.0, 2.0)
-    mix = jnp.where(from_step == to_step, single, jnp.where(jnp.abs(from_step - to_step) == 1, -1.0, 0.0))
-    const = jnp.where(to_step == 0, 0.0, jnp.where(lax.rem(to_step, 2) == 1, -single, 2.0))
+    def second_difference(shift):
+        from_step = iota((WIDTH, BINS), 0) // GROUPS
+        bin_of = iota((WIDTH, BINS), 1) - shift
+        digit = jnp.floor((bin_of.astype(F32) + 0.5) * (1.0 / FINE)).astype(jnp.int32)
+        to_step = bin_of - FINE * digit
+        single = jnp.where(to_step == FINE - 1, 1.0, 2.0)
+        mix = jnp.where(from_step == to_step, single, jnp.where(jnp.abs(from_step - to_step) == 1, -1.0, 0.0))
+        const = jnp.where(to_step == 0, 0.0, jnp.where(lax.rem(to_step, 2) == 1, -single, 2.0))
+        return jnp.where(from_step == 0, const, mix).astype(BF16)
+
     r, c = iota((128, 128), 0), iota((128, 128), 1)
     same = jnp.logical_and(r // 8 == c // 8, (lax.rem(r, 8) < 4) != (lax.rem(c, 8) < 4))
     taps = jnp.where(same, tap(r - c), 0.0).astype(BF16)
     cross[...] = jnp.concatenate([taps, taps], axis=0)
-    unit[...] = jnp.where(from_step == 0, const, mix).astype(BF16)
+    for i in range(2):
+        unit[:, BINS * i : BINS * (i + 1)] = second_difference(i)
 
     lower = first_ref[...].astype(F32) - 1.0
     upper = beyond_ref[...].astype(F32)
@@ -198,8 +205,8 @@
     def slant(pairs):
         total_ = None
         for c, (ahead_, behind) in zip(COEFS, pairs):
-            term = c * (ahead_ - behind)
-            total_ = term if total_ is None else total_ + term
+            term = ahead_ - behind
+            total_ = term if total_ is None else total_ + (c / COEFS[0]) * term
         return total_
 
     steps = range(1, len(COEFS) + 1)
@@ -219,7 +226,7 @@
         return g * g
 
     def length(gx, rest):
-        s = (rest + gx * gx) + 1.0
+        s = (rest + gx * gx) * COEFS[0] ** 2 + 1.0
         return s * lax.rsqrt(s) - 1.0
 
     def classes(m, offset):
@@ -301,13 +308,6 @@
 
     inside = list(range(4, nz - 4))
     count = nz // planes
-    outside = [z for z in range(nz) if z not in inside]
-    for t in range(tiles):
-        edge_row = t in (0, tiles - 1)
-        for z in inside if edge_row else ():
-            prepare(z, t, along_z)
-        for z in outside:
-            prepare(z, t, None if edge_row else along_y)
     gathered = [None] * (planes * tiles)
     for i in range(planes * tiles):
         u, t = i // tiles, i % tiles
@@ -320,7 +320,13 @@
     to_left[...] = jnp.where(low_four, pltpu.roll(upper_half, 124, 1), lower_half)
     x_low.start()
     x_high.start()
-
+    outside = [z for z in range(nz) if z not in inside]
+    for t in range(tiles):
+        edge_row = t in (0, tiles - 1)
+        for z in inside if edge_row else ():
+            prepare(z, t, along_z)
+        for z in outside:
+            prepare(z, t, None if edge_row else along_y)
     inner = [
         tally_up([deferred(z, t, None, along_y, along_z) for z in inside for t in range(1, tiles - 1)], True)
     ]
@@ -336,22 +342,25 @@
     ext[own, 8 + ny : 12 + ny, :] = from_above[...]
     inner.append(tally_up([deferred(z, t, True, along_y) for z in inside for t in (0, tiles - 1)]))
     fold([(2, count - 2)], (0, tiles - 1))
-    for c in z_sends:
-        c.wait()
-    inner.append(
-        tally_up(
-            [
-                deferred(z, t, False, along_y, along_z)
-                if t in (0, tiles - 1)
-                else deferred(z, t, True, along_z)
-                for z in outside
-                for t in range(tiles)
-            ]
-        )
-    )
+    for sends, pair in ((z_near, (2, 3, nz - 4, nz - 3)), (z_far, (0, 1, nz - 2, nz - 1))):
+        for c in sends:
+            c.wait()
+        inner.append(
+            tally_up(
+                [
+                    deferred(z, t, False, along_y, along_z)
+                    if t in (0, tiles - 1)
+                    else deferred(z, t, True, along_z)
+                    for z in pair
+                    for t in range(tiles)
+                ]
+            )
+        )
     fold([(0, 2), (count - 2, count)], range(tiles))
     inner = functools.reduce(merge, inner)
 
+    hear("gy", ready_y, 1)
+    tell("gy", ready_y, y_hops, 2)
     x_low.wait()
     x_high.wait()
     left_rim, right_rim = from_left[...], from_right[...]
@@ -369,7 +378,7 @@
     extra_lo = (extra - extra_hi.astype(F32)).astype(BF16)
     corr = jnp.dot(
         jnp.concatenate([extra_hi, extra_lo], axis=1), cross[...], preferred_element_type=F32
-    ) * (1.0 / SCALE)
+    ) * (1.0 / (SCALE * COEFS[0]))
     rim = []
     for i in range(planes * tiles):
         at = slice(8 * i, 8 * i + 8)
@@ -396,27 +405,30 @@
     def by_class(a):
         return jnp.sum(jnp.where(keep[None], a.reshape(COARSE, GROUPS, WIDTH), 0.0), axis=1)
 
-    sums = jnp.concatenate([by_class(tally[0:SPAN, :]), by_class(tally[SPAN : 2 * SPAN, :])], axis=0)
-    high = sums.astype(BF16)
-    rest = sums - high.astype(F32)
-    middle_bits = rest.astype(BF16)
-    low_bits = (rest - middle_bits.astype(F32)).astype(BF16)
+    parts = by_class(tally[SPAN : 2 * SPAN, :])
+    sums = jnp.concatenate([by_class(tally[0:SPAN, :]) - parts, parts], axis=0)
+    high = sums.astype(BF16).astype(F32)
+    mid = (sums - high).astype(BF16).astype(F32)
+    tail = sums - high - mid
     three = jnp.dot(
-        jnp.concatenate([high.astype(F32), middle_bits.astype(F32), low_bits.astype(F32)], axis=0).astype(BF16),
-        unit[...],
-        preferred_element_type=F32,
+        jnp.concatenate([high, mid, tail], axis=0).astype(BF16), unit[...], preferred_element_type=F32
     )
     n = 2 * COARSE
     both = (three[2 * n : 3 * n] + three[n : 2 * n]) + three[0:n]
-    place = iota((2 * COARSE, BINS), 1).astype(F32)
-    digit = jnp.floor((place + 0.5) * (1.0 / FINE)).astype(jnp.int32)
-    both = jnp.where(lax.rem(iota((2 * COARSE, BINS), 0), COARSE) == digit, both, 0.0)
-    low_sum = jnp.sum(both[0:COARSE, :], axis=0, keepdims=True)
-    part = jnp.sum(both[COARSE : 2 * COARSE, :], axis=0, keepdims=True)
+    class_of = iota((COARSE, BINS), 0)
+
+    def at_home(shift):
+        bins = (iota((COARSE, BINS), 1) - shift).astype(F32)
+        return class_of == jnp.floor((bins + 0.5) * (1.0 / FINE)).astype(jnp.int32)
+
+    bins = jnp.sum(
+        jnp.where(at_home(0), both[0:COARSE, 0:BINS], 0.0)
+        + jnp.where(at_home(1), both[COARSE:n, BINS : 2 * BINS], 0.0),
+        axis=0,
+        keepdims=True,
+    )
+    row0, row1 = bins[:, 0:128], bins[:, 128:256]
     lane1 = iota((1, 128), 1)
-    turned = [pltpu.roll(part[:, 0:128], 1, 1), pltpu.roll(part[:, 128:256], 1, 1)]
-    row0 = low_sum[:, 0:128] - part[:, 0:128] + jnp.where(lane1 == 0, turned[1], turned[0])
-    row1 = low_sum[:, 128:256] - part[:, 128:256] + jnp.where(lane1 == 0, turned[0], turned[1])
 
     def all_of(op, a):
         return op(op(a, axis=0, keepdims=True), axis=1, keepdims=True)
@@ -485,7 +497,7 @@
         put_rims,
     )
     gather_far[far] = row
-    hear("gy", ready_y, 1)
+    hear("gy", ready_y, 2)
     row = share(gather_far, far, [{"gy": ahead["gy", dy]} for dy in by_distance(sizes["gy"]) if dy], 1)
     cells = nz * ny * nx * total
     hist_ref[...] = row[0:2] * (BINS / cells)
@@ -536,14 +548,14 @@
                 pltpu.VMEM((2 * ny, 128), F32),
                 pltpu.VMEM((2 * ny, 128), F32),
                 pltpu.VMEM((2, 2 * SPAN, WIDTH), F32),
-                pltpu.VMEM((WIDTH, BINS), BF16),
+                pltpu.VMEM((WIDTH, 2 * BINS), BF16),
                 pltpu.VMEM((sizes["gx"] * sizes["gz"], 3, 128), F32),
                 pltpu.VMEM((sizes["gy"], 3, 128), F32),
                 pltpu.SemaphoreType.DMA((4,)),
-                pltpu.SemaphoreType.DMA((6,)),
-                pltpu.SemaphoreType.DMA((6,)),
-                pltpu.SemaphoreType.REGULAR((2,)),
-                pltpu.SemaphoreType.REGULAR((2,)),
+                pltpu.SemaphoreType.DMA((8,)),
+                pltpu.SemaphoreType.DMA((8,)),
+                pltpu.SemaphoreType.REGULAR((3,)),
+                pltpu.SemaphoreType.REGULAR((3,)),
                 pltpu.SemaphoreType.DMA((2,)),
                 pltpu.SemaphoreType.DMA((2,)),
             ],

time: 36.4 us -> 36.1 us (level)
    pallas_call x1, Pallas kernels: 33.3 us -> 33 us  [on_device(): pl.pallas_call(functools.partial(kernel, sizes), out_shape=results, in_sp...]
where the time goes in v4:
time: 36.1 us; the launch traced here: 35.9 us
  Pallas kernels  34 us (94%)
  between operations  1.93 us (5%)
    pallas_call x1, Pallas kernels, on_device(): pl.pallas_call(functools.partial(kernel, sizes), out_shape=results, in_sp...  33 us
    pallas_call x1, Pallas kernels, on_device(): pl.pallas_call(finish, out_shape=results, in_specs=[vmem, vmem, vmem], ou...  1 us

profile of v4, /device:TPU:1, one launch (start us, length us, event | category | flops | bytes accessed | tf_op | source)
XLA Modules:
  0.0 35.9 jit_solution(2585504180284301104)
XLA Ops:
  1.9 33.0 %shard_map.58 = (f32[32,64,128]{2,1,0:T(8,128)S(1)}, f32[2,128]{1,0:T(2,128)S(1)}, f32[1,4]{1,0:T(1,128)S(1)}) custom-call(s32[1,1]{1,0:T(1,128)} %bitcast.4.first_ref, s32[1,1]{1,0:T(1,128)} %bitcast.5.beyond_ref, f32[32,64,128]{2,1,0:T(8,128)} %x_ref.1), custom_call_target="tpu_custom_call" | custom-call | tf_op jit(solution)/shard_map/pallas_call | solution.py:528
  34.9 1.0 %shard_map.59 = (f32[32,64,128]{2,1,0:T(8,128)}, f32[2,128]{1,0:T(2,128)}, f32[1,4]{1,0:T(1,128)}) custom-call(f32[32,64,128]{2,1,0:T(8,128)S(1)} %get-tuple-element.9.refs_0_, f32[2,128]{1,0:T(2,128)S(1)} %get-tuple-element.10.refs_1_, f32[1,4]{1,0:T(1,128)S(1)} %get-tuple-element.11.refs_2_), custom_call_target="tpu_custom_call" | custom-call | tf_op jit(solution)/shard_map/pallas_call | solution.py:566
